TPU v7x, 32 devices: a whole 2x2x4 slice. The times are simulated.
32 devices in a mesh: rows: 8 (over z, x), cols: 4 (over y, core).
Axes of the slice: x: 2, y: 2, z: 4, core: 2. Of those that a mesh axis runs over, the one named last changes fastest.
Arguments:
- basis: float32 [8192, 4096], P('rows', 'cols'), may hold values from -119.66257 to 119.66257, as said below
- block: float32 [8192, 512], P('rows', 'cols'), may hold values from -1800 to 1800
Outputs:
- ortho: float32 [8192, 512], P('rows', 'cols')
- factors: float32 [4, 128, 128], P('cols')
Inputs may be any that keep to these rules, and one draw needn't show every extreme that they name: Under the inner product (sum over rows divided by 8192) the basis columns have squared norms between 0.6 and 1.9, and inner products of distinct basis columns are at most 0.05 in magnitude.
All inputs are finite; a program needn't handle non-finite values.
Results may differ from a plain program's by a relative error of at most 0.000076.
Values sent between devices are 32-bit elements; how exact they have to be, the bound alone decides.
No kernel may reach another device: no remote copies, remote signals or barrier semaphores. Data moves between devices by JAX's collectives and lax.ppermute only.
A program may use at most 64 MiB of HBM per device.

v0:
```python
import jax
import jax.numpy as jnp
from jax import lax
from jax.sharding import PartitionSpec as P

BLK = 128


def solve_block(lower_factor, vectors):
    return jax.scipy.linalg.solve_triangular(lower_factor, vectors, lower=True)


def body(basis, block):
    highest = lax.Precision.HIGHEST
    local_rows = basis.shape[0]
    inverse = 1.0 / (local_rows * lax.axis_size("rows"))
    width = block.shape[1]
    column_index = lax.axis_index("cols")

    def project(piece):
        return (
            lax.dot_general(
                basis,
                piece,
                (((0,), (0,)), ((), ())),
                precision=highest,
                preferred_element_type=jnp.float32,
            )
            * inverse
        )

    def expand(coef):
        return jnp.dot(basis, coef, precision=highest, preferred_element_type=jnp.float32)

    terms_one = project(lax.all_gather(block, "cols", axis=1, tiled=True))
    coef_one = lax.psum(terms_one, "rows")
    placed = lax.dynamic_update_slice_in_dim(
        jnp.zeros((local_rows, coef_one.shape[1]), jnp.float32), block, column_index * width, 1
    )
    first_whole = lax.psum(placed - expand(coef_one), "cols")
    terms_two = project(first_whole)
    first = lax.dynamic_slice_in_dim(first_whole, column_index * width, width, 1)
    coef_two = lax.psum(terms_two, "rows")
    second = first - lax.psum_scatter(expand(coef_two), "cols", scatter_dimension=1, tiled=True)
    blocks = width // BLK
    pieces = second.reshape(local_rows, blocks, BLK)
    gram = jnp.einsum("mbi,mbj->bij", pieces, pieces, precision=highest) * inverse
    gram = lax.psum(gram, "rows")
    lower_factor = jnp.linalg.cholesky(gram)
    solved = jax.vmap(solve_block)(lower_factor, jnp.transpose(pieces, (1, 2, 0)))
    ortho = jnp.transpose(solved, (2, 0, 1)).reshape(local_rows, width)
    return (ortho, jnp.transpose(lower_factor, (0, 2, 1)))


def solution(mesh):
    placed = (P("rows", "cols"), P("rows", "cols"))
    return jax.shard_map(
        body,
        mesh=mesh,
        in_specs=placed,
        out_specs=(P("rows", "cols"), P("cols", None, None)),
        check_vma=False,
    )
```

profile of v0, /device:TPU:0, one launch (start us, length us, event | category | flops | bytes accessed | tf_op | source)
XLA Modules:
  0.0 476.0 jit_solution(7517272405939530119)
XLA Ops:
  7.2 0.0 all-gather.2.cloned.1.call-start
  7.2 0.7 all-gather.2.cloned.1.call-update
  7.9 0.0 all-reduce.5.cloned.1.call-start
  7.9 27.2 %all-gather.2.cloned.1.call-done = f32[1024,512]{1,0:T(8,128)} async-done(((f32[1024,128]{1,0:T(8,128)}), f32[1024,512]{1,0:T(8,128)}) %all-gather.2.cloned.1.call-update) | async-done | bytes 2097168 | tf_op jit(solution)/shard_map/all_gather | solution.py:35
  35.1 10.2 %convolution_multiply_fusion = f32[1024,512]{1,0:T(8,128)} fusion(f32[1024,1024]{1,0:T(8,128)} %param.2, f32[1024,512]{1,0:T(8,128)} %all-gather.2.cloned.1.call-done), kind=kOutput, calls=%fused_computation.3 | convolution fusion | flops 6442975232 | bytes 8388608 | tf_op jit(solution)/shard_map/dot_general | solution.py:22
  45.3 0.0 copy-start.1
  45.3 0.0 all-reduce.5.cloned.1.call-update
  45.3 0.0 all-reduce.7.cloned.1.call-start
  45.4 1.0 copy-done.1
  46.3 0.2 copy.4
  46.5 0.2 broadcast_in_dim.7
  46.8 0.1 constant_dynamic-update-slice_fusion
  46.8 100.9 %all-reduce.5.cloned.1.call-done = f32[1024,512]{1,0:T(8,128)} async-done(((f32[1024,512]{1,0:T(8,128)}), f32[1024,512]{1,0:T(8,128)}) %all-reduce.5.cloned.1.call-update) | async-done | bytes 2097168 | tf_op jit(solution)/shard_map/psum | solution.py:36
  147.8 16.7 %bitcast_subtract_fusion = f32[1024,512]{0,1:T(8,128)} fusion(f32[1024,512]{0,1:T(8,128)S(1)} %constant_dynamic-update-slice_fusion, f32[1024,512]{1,0:T(8,128)} %all-reduce.5.cloned.1.call-done, f32[1024,1024]{1,0:T(8,128)} %param.2), kind=kOutput, calls=%fused_computation | convolution fusion | flops 6442975232 | bytes 10485760 | tf_op jit(solution)/shard_map/dot_general | solution.py:33
  164.5 0.0 all-reduce.7.cloned.1.call-update
  164.5 0.2 all-reduce.9.cloned.1.call-start
  164.7 50.6 %all-reduce.7.cloned.1.call-done = f32[1024,512]{0,1:T(8,128)} async-done(((f32[1024,512]{0,1:T(8,128)}), f32[1024,512]{0,1:T(8,128)}) %all-reduce.7.cloned.1.call-update) | async-done | bytes 2097168 | tf_op jit(solution)/shard_map/psum | solution.py:40
  215.3 10.2 %multiply_bitcast_fusion = f32[1024,512]{0,1:T(8,128)} fusion(f32[1024,512]{0,1:T(8,128)} %all-reduce.7.cloned.1.call-done, f32[1024,1024]{1,0:T(8,128)} %param.2), kind=kOutput, calls=%fused_computation.1 | convolution fusion | flops 6442975232 | bytes 8388608 | tf_op jit(solution)/shard_map/dot_general | solution.py:22
  225.6 0.0 all-reduce.9.cloned.1.call-update
  225.6 0.0 reduce-scatter.2.cloned.1.call-start
  225.6 102.5 %all-reduce.9.cloned.1.call-done = f32[1024,512]{0,1:T(8,128)} async-done(((f32[1024,512]{0,1:T(8,128)}), f32[1024,512]{0,1:T(8,128)}) %all-reduce.9.cloned.1.call-update) | async-done | bytes 2097168 | tf_op jit(solution)/shard_map/psum | solution.py:43
  328.1 10.3 %convolution_bitcast_fusion = f32[1024,512]{0,1:T(8,128)} fusion(f32[1024,512]{0,1:T(8,128)} %all-reduce.9.cloned.1.call-done, f32[1024,1024]{1,0:T(8,128)} %param.2), kind=kOutput, calls=%fused_computation.2 | convolution fusion | flops 6442450944 | bytes 8388608 | tf_op jit(solution)/shard_map/dot_general | solution.py:33
  338.4 0.0 copy-start
  338.4 0.0 reduce-scatter.2.cloned.1.call-update
  338.4 0.3 all-reduce.11.cloned.1.call-start
  338.7 30.3 %reduce-scatter.2.cloned.1.call-done = f32[1024,128]{0,1:T(8,128)} async-done(((f32[1024,512]{0,1:T(8,128)}), f32[1024,128]{0,1:T(8,128)}) %reduce-scatter.2.cloned.1.call-update) | async-done | bytes 524304 | tf_op jit(solution)/shard_map/reduce_scatter | solution.py:44
  369.0 0.0 copy-done
  369.0 0.0 copy-start.2
  369.0 2.5 fusion
  371.5 0.0 all-reduce.11.cloned.1.call-update
  371.5 70.6 %all-reduce.11.cloned.1.call-done = f32[1,128,128]{1,2,0:T(8,128)} async-done(((f32[1,128,128]{1,2,0:T(8,128)}), f32[1,128,128]{1,2,0:T(8,128)}) %all-reduce.11.cloned.1.call-update) | async-done | bytes 65552 | tf_op jit(solution)/shard_map/psum | solution.py:48
  442.2 0.9 copy.6
  443.1 0.9 fusion.3
  444.0 11.7 %custom-call.8 = f32[1,128,128]{2,1,0:T(8,128)S(1)} custom-call(f32[1,128,128]{2,1,0:T(8,128)S(1)} %fusion.3), custom_call_target="Cholesky" | custom-call | tf_op jit(solution)/shard_map/jit(cholesky)/cholesky | solution.py:49
  455.7 0.6 compare_reduce_fusion
  456.4 0.7 fusion.4
  457.0 9.8 %custom-call.9 = f32[1,1,128,128]{2,3,1,0:T(8,128)S(1)} custom-call(f32[1,1,128,128]{3,2,1,0:T(8,128)S(1)} %get-tuple-element.5), custom_call_target="InvertDiagBlocksLowerTriangular" | custom-call | tf_op jit(solution)/shard_map/vmap(jit(_solve_triangular))/triangular_solve | solution.py:10
  466.8 0.0 copy-done.2
  466.8 0.6 convolution_bitcast_fusion.1
  467.5 1.0 copy.7
  468.5 0.7 copy.8
  (1 shorter events, 0.0 us)
Async XLA Ops:
  7.2 27.9 %all-gather.2.cloned.1.call-start = ((), (), s32[]{:S(2)}) async-start(), calls=%async_computation.1 | async-start | bytes 2621440 | tf_op jit(solution)/shard_map/all_gather | solution.py:35
  7.9 139.9 %all-reduce.5.cloned.1.call-start = ((), (), s32[]{:S(2)}) async-start(), calls=%async_computation.2 | async-start | bytes 4194304 | tf_op jit(solution)/shard_map/psum | solution.py:36
  45.3 1.0 copy-start.1
  45.3 170.0 %all-reduce.7.cloned.1.call-start = ((), (), s32[]{:S(2)}) async-start(), calls=%async_computation.3 | async-start | bytes 4194304 | tf_op jit(solution)/shard_map/psum | solution.py:40
  164.5 163.6 %all-reduce.9.cloned.1.call-start = ((), (), s32[]{:S(2)}) async-start(), calls=%async_computation.4 | async-start | bytes 4194304 | tf_op jit(solution)/shard_map/psum | solution.py:43
  225.6 143.4 %reduce-scatter.2.cloned.1.call-start = ((), (), s32[]{:S(2)}) async-start(), calls=%async_computation.5 | async-start | bytes 2621440 | tf_op jit(solution)/shard_map/reduce_scatter | solution.py:44
  338.4 30.6 %copy-start = (f32[1024,512]{0,1:T(8,128)S(1)}, f32[1024,512]{0,1:T(8,128)}, u32[]{:S(2)}) copy-start(f32[1024,512]{0,1:T(8,128)} %all-reduce.7.cloned.1.call-done) | copy-start | bytes 6291460
  338.4 103.8 %all-reduce.11.cloned.1.call-start = ((), (), s32[]{:S(2)}) async-start(), calls=%async_computation.6 | async-start | bytes 131072 | tf_op jit(solution)/shard_map/psum | solution.py:48
  369.0 97.8 %copy-start.2 = (f32[1024,128]{0,1:T(8,128)S(1)}, f32[1024,128]{0,1:T(8,128)}, u32[]{:S(2)}) copy-start(f32[1024,128]{0,1:T(8,128)} %reduce-scatter.2.cloned.1.call-done) | copy-start | bytes 1572868
Sparse Core Ops, SparseCore 0:
  9.5 25.5 all-gather.1
  45.4 102.3 all-reduce.4
  164.6 50.6 all-reduce.6
  225.7 102.3 all-reduce.8
  338.5 30.4 reduce-scatter.1
  372.9 69.2 all-reduce.10
where the time goes:
time: 476 us
  waiting for transfers between devices  383 us (80%)
  matrix products  50.5 us (11%)
  other arithmetic  23.7 us (5%)
  between operations  14.2 us (3%)
    psum x1, waiting for transfers between devices, body(): coef_two = lax.psum(terms_two, 'rows')  102 us
    psum x1, waiting for transfers between devices, body(): coef_one = lax.psum(terms_one, 'rows')  101 us
    psum x1, waiting for transfers between devices, body(): gram = lax.psum(gram, 'rows')  70.6 us
    psum x1, waiting for transfers between devices, body(): first_whole = lax.psum(placed - expand(coef_one), 'cols')  50.6 us
    reduce_scatter x1, waiting for transfers between devices, body(): lax.psum_scatter(expand(coef_two), 'cols', scatter_dimension=1, tiled=True)  30.3 us
    all_gather x1, waiting for transfers between devices, body(): terms_one = project(lax.all_gather(block, 'cols', axis=1, tiled=True))  27.2 us
    dot_general x2, matrix products, expand(): jnp.dot(basis, coef, precision=highest, preferred_element_type=jnp.float32)  27 us
    dot_general x2, matrix products, project(): lax.dot_general(basis, piece, (((0,), (0,)), ((), ())), precision=highest...  20.4 us
  transfers between devices with their start and end apart: 6, of which 6 were waited for; matrix products, arithmetic and copies ran while one was open for 0% of the time, Pallas kernels for 0%

commit v1 on v0

--- a/solution.py
+++ b/solution.py
@@ -45,7 +45,7 @@
     blocks = width // BLK
     pieces = second.reshape(local_rows, blocks, BLK)
     gram = jnp.einsum("mbi,mbj->bij", pieces, pieces, precision=highest) * inverse
-    gram = lax.psum(gram, "rows")
+    gram = jnp.sum(lax.all_gather(gram, "rows"), axis=0)
     lower_factor = jnp.linalg.cholesky(gram)
     solved = jax.vmap(solve_block)(lower_factor, jnp.transpose(pieces, (1, 2, 0)))
     ortho = jnp.transpose(solved, (2, 0, 1)).reshape(local_rows, width)

time: 476 us -> 435 us (0.914)
  waiting for transfers between devices: 383 us -> 312 us
  blocking collectives: 0 us -> 31.8 us
    psum x1 -> x0, waiting for transfers between devices: 70.6 us -> none  [body(): gram = lax.psum(gram, 'rows')]
    all_gather x0 -> x1, blocking collectives: none -> 31.8 us  [body(): gram = jnp.sum(lax.all_gather(gram, 'rows'), axis=0)]
  transfers between devices with their start and end apart: 6 -> 5, of which waited for: 6 -> 5; matrix products, arithmetic and copies ran while one was open for 0% -> 0% of each run, Pallas kernels for 0% -> 0%
where the time goes in v1:
time: 435 us
  waiting for transfers between devices  312 us (72%)
  matrix products  49.9 us (11%)
  blocking collectives  31.8 us (7%)
  other arithmetic  22.9 us (5%)
  between operations  13.9 us (3%)
    psum x1, waiting for transfers between devices, body(): coef_two = lax.psum(terms_two, 'rows')  102 us
    psum x1, waiting for transfers between devices, body(): coef_one = lax.psum(terms_one, 'rows')  101 us
    psum x1, waiting for transfers between devices, body(): first_whole = lax.psum(placed - expand(coef_one), 'cols')  50.6 us
    all_gather x1, blocking collectives, body(): gram = jnp.sum(lax.all_gather(gram, 'rows'), axis=0)  31.8 us
    reduce_scatter x1, waiting for transfers between devices, body(): lax.psum_scatter(expand(coef_two), 'cols', scatter_dimension=1, tiled=True)  30.6 us
    all_gather x1, waiting for transfers between devices, body(): terms_one = project(lax.all_gather(block, 'cols', axis=1, tiled=True))  27.2 us
    dot_general x2, matrix products, expand(): jnp.dot(basis, coef, precision=highest, preferred_element_type=jnp.float32)  27 us
    dot_general x2, matrix products, project(): lax.dot_general(basis, piece, (((0,), (0,)), ((), ())), precision=highest...  20.4 us
  transfers between devices with their start and end apart: 5, of which 5 were waited for; matrix products, arithmetic and copies ran while one was open for 0% of the time, Pallas kernels for 0%

profile of v1, /device:TPU:0, one launch (start us, length us, event | category | flops | bytes accessed | tf_op | source)
XLA Modules:
  0.0 434.7 jit_solution(803231580015927333)
XLA Ops:
  7.2 0.0 all-gather.3.cloned.1.call-start
  7.2 0.7 all-gather.3.cloned.1.call-update
  7.9 0.0 all-reduce.4.cloned.1.call-start
  7.9 27.2 %all-gather.3.cloned.1.call-done = f32[1024,512]{1,0:T(8,128)} async-done(((f32[1024,128]{1,0:T(8,128)}), f32[1024,512]{1,0:T(8,128)}) %all-gather.3.cloned.1.call-update) | async-done | bytes 2097168 | tf_op jit(solution)/shard_map/all_gather | solution.py:35
  35.1 10.2 %convolution_multiply_fusion = f32[1024,512]{1,0:T(8,128)} fusion(f32[1024,1024]{1,0:T(8,128)} %param.2, f32[1024,512]{1,0:T(8,128)} %all-gather.3.cloned.1.call-done), kind=kOutput, calls=%fused_computation.3 | convolution fusion | flops 6442975232 | bytes 8388608 | tf_op jit(solution)/shard_map/dot_general | solution.py:22
  45.3 0.0 copy-start.1
  45.3 0.0 all-reduce.4.cloned.1.call-update
  45.3 0.0 all-reduce.6.cloned.1.call-start
  45.4 1.0 copy-done.1
  46.3 0.2 copy.8
  46.5 0.2 broadcast_in_dim.7
  46.8 0.1 constant_dynamic-update-slice_fusion
  46.9 100.9 %all-reduce.4.cloned.1.call-done = f32[1024,512]{1,0:T(8,128)} async-done(((f32[1024,512]{1,0:T(8,128)}), f32[1024,512]{1,0:T(8,128)}) %all-reduce.4.cloned.1.call-update) | async-done | bytes 2097168 | tf_op jit(solution)/shard_map/psum | solution.py:36
  147.8 16.7 %bitcast_subtract_fusion = f32[1024,512]{0,1:T(8,128)} fusion(f32[1024,512]{0,1:T(8,128)S(1)} %constant_dynamic-update-slice_fusion, f32[1024,512]{1,0:T(8,128)} %all-reduce.4.cloned.1.call-done, f32[1024,1024]{1,0:T(8,128)} %param.2), kind=kOutput, calls=%fused_computation | convolution fusion | flops 6442975232 | bytes 10485760 | tf_op jit(solution)/shard_map/dot_general | solution.py:33
  164.4 0.0 all-reduce.6.cloned.1.call-update
  164.5 0.2 all-reduce.8.cloned.1.call-start
  164.7 50.6 %all-reduce.6.cloned.1.call-done = f32[1024,512]{0,1:T(8,128)} async-done(((f32[1024,512]{0,1:T(8,128)}), f32[1024,512]{0,1:T(8,128)}) %all-reduce.6.cloned.1.call-update) | async-done | bytes 2097168 | tf_op jit(solution)/shard_map/psum | solution.py:40
  215.3 10.3 %multiply_bitcast_fusion = f32[1024,512]{0,1:T(8,128)} fusion(f32[1024,512]{0,1:T(8,128)} %all-reduce.6.cloned.1.call-done, f32[1024,1024]{1,0:T(8,128)} %param.2), kind=kOutput, calls=%fused_computation.1 | convolution fusion | flops 6442975232 | bytes 8388608 | tf_op jit(solution)/shard_map/dot_general | solution.py:22
  225.5 0.0 all-reduce.8.cloned.1.call-update
  225.6 0.0 reduce-scatter.2.cloned.1.call-start
  225.6 102.5 %all-reduce.8.cloned.1.call-done = f32[1024,512]{0,1:T(8,128)} async-done(((f32[1024,512]{0,1:T(8,128)}), f32[1024,512]{0,1:T(8,128)}) %all-reduce.8.cloned.1.call-update) | async-done | bytes 2097168 | tf_op jit(solution)/shard_map/psum | solution.py:43
  328.1 10.3 %convolution_bitcast_fusion = f32[1024,512]{0,1:T(8,128)} fusion(f32[1024,512]{0,1:T(8,128)} %all-reduce.8.cloned.1.call-done, f32[1024,1024]{1,0:T(8,128)} %param.2), kind=kOutput, calls=%fused_computation.2 | convolution fusion | flops 6442450944 | bytes 8388608 | tf_op jit(solution)/shard_map/dot_general | solution.py:33
  338.4 0.0 copy-start
  338.4 0.0 reduce-scatter.2.cloned.1.call-update
  338.4 30.6 %reduce-scatter.2.cloned.1.call-done = f32[1024,128]{0,1:T(8,128)} async-done(((f32[1024,512]{0,1:T(8,128)}), f32[1024,128]{0,1:T(8,128)}) %reduce-scatter.2.cloned.1.call-update) | async-done | bytes 524304 | tf_op jit(solution)/shard_map/reduce_scatter | solution.py:44
  369.0 0.0 copy-done
  369.0 0.0 copy-start.2
  369.0 1.9 convolution_multiply_fusion.1
  370.9 31.8 %all-gather = f32[1024,128]{1,0:T(8,128)S(1)} all-gather(f32[128,128]{1,0:T(8,128)S(1)} %convolution_multiply_fusion.1), channel_id=2, replica_groups=mesh['rows'=8,'cols'=4] {'rows'}, dimensions={0}, use_global_device_ids=true | all-gather | bytes 589824 | tf_op jit(solution)/shard_map/all_gather | solution.py:48
  402.7 0.1 copy.9
  402.8 0.1 copy.10
  402.9 11.7 %custom-call.8 = f32[1,128,128]{2,1,0:T(8,128)S(1)} custom-call(f32[1,128,128]{2,1,0:T(8,128)S(1)} %fusion.1), custom_call_target="Cholesky" | custom-call | tf_op jit(solution)/shard_map/jit(cholesky)/cholesky | solution.py:49
  414.6 0.6 compare_reduce_fusion
  415.3 0.7 fusion.3
  415.9 9.8 %custom-call.9 = f32[1,1,128,128]{2,3,1,0:T(8,128)S(1)} custom-call(f32[1,1,128,128]{3,2,1,0:T(8,128)S(1)} %get-tuple-element.7), custom_call_target="InvertDiagBlocksLowerTriangular" | custom-call | tf_op jit(solution)/shard_map/vmap(jit(_solve_triangular))/triangular_solve | solution.py:10
  425.8 0.0 copy-done.2
  425.8 0.6 convolution_bitcast_fusion.1
  426.4 1.0 copy.11
  427.4 0.7 copy.12
  (3 shorter events, 0.1 us)
Async XLA Ops:
  7.2 27.9 %all-gather.3.cloned.1.call-start = ((), (), s32[]{:S(2)}) async-start(), calls=%async_computation.1 | async-start | bytes 2621440 | tf_op jit(solution)/shard_map/all_gather | solution.py:35
  7.9 139.9 %all-reduce.4.cloned.1.call-start = ((), (), s32[]{:S(2)}) async-start(), calls=%async_computation.2 | async-start | bytes 4194304 | tf_op jit(solution)/shard_map/psum | solution.py:36
  45.3 1.0 copy-start.1
  45.3 170.0 %all-reduce.6.cloned.1.call-start = ((), (), s32[]{:S(2)}) async-start(), calls=%async_computation.3 | async-start | bytes 4194304 | tf_op jit(solution)/shard_map/psum | solution.py:40
  164.5 163.6 %all-reduce.8.cloned.1.call-start = ((), (), s32[]{:S(2)}) async-start(), calls=%async_computation.4 | async-start | bytes 4194304 | tf_op jit(solution)/shard_map/psum | solution.py:43
  225.6 143.4 %reduce-scatter.2.cloned.1.call-start = ((), (), s32[]{:S(2)}) async-start(), calls=%async_computation.5 | async-start | bytes 2621440 | tf_op jit(solution)/shard_map/reduce_scatter | solution.py:44
  338.4 30.6 %copy-start = (f32[1024,512]{0,1:T(8,128)S(1)}, f32[1024,512]{0,1:T(8,128)}, u32[]{:S(2)}) copy-start(f32[1024,512]{0,1:T(8,128)} %all-reduce.6.cloned.1.call-done) | copy-start | bytes 6291460
  369.0 56.8 %copy-start.2 = (f32[1024,128]{0,1:T(8,128)S(1)}, f32[1024,128]{0,1:T(8,128)}, u32[]{:S(2)}) copy-start(f32[1024,128]{0,1:T(8,128)} %reduce-scatter.2.cloned.1.call-done) | copy-start | bytes 1572868
Sparse Core Ops, SparseCore 0:
  9.5 25.5 all-gather.2
  45.4 102.2 all-reduce.3
  164.6 50.6 all-reduce.5
  225.7 102.3 all-reduce.7
  338.5 30.4 reduce-scatter.1
